TPU v7x, 32 devices: a whole 2x2x4 slice. The times are simulated.
32 devices in a mesh: kx: 2 (over x), ky: 4 (over y, core), kz: 4 (over z).
Axes of the slice: x: 2, y: 2, z: 4, core: 2. Of those that a mesh axis runs over, the one named last changes fastest.
Arguments:
- coefficients: bfloat16 [2, 2, 4, 4, 512, 2048], P(None, 'kx', 'ky', 'kz'), may hold values from -1 to 1
- shift_blocks: int32 [3], replicated, may hold values from 1 to 15, as said below
Outputs:
- centre: float32 [3, 512], replicated
- spread: float32 [3, 512], replicated
- coherence: float32 [3, 2, 4, 4], P(None, 'kx', 'ky', 'kz')
Inputs may be any that keep to these rules, and one draw needn't show every extreme that they name: The coefficients one period further along direction d are those of the first k-point of the string with plane-wave index g read at (g + 128 * shift_blocks[d]) mod 2048.
All inputs are finite; a program needn't handle non-finite values.
Results may differ from a plain program's by a relative error of at most 0.0003.
Values may be sent and summed in bfloat16 or wider, within the bound.
No kernel may reach another device: no remote copies, remote signals or barrier semaphores. Data moves between devices by JAX's collectives and lax.ppermute only.
A program may use at most 128 MiB of HBM per device.

v0:
```python
import jax
import jax.numpy as jnp
from jax import lax
from jax.sharding import PartitionSpec as P


def passed_along(value, axis, steps):
    count = lax.axis_size(axis)
    pairs = [(source, (source + steps) % count) for source in range(count)]
    return lax.ppermute(value, axis, pairs)


def pair_measure(own_point, partner):
    bands = own_point.shape[1]
    left_side = jnp.concatenate([own_point[0], own_point[1]], axis=1)
    right_side = jnp.concatenate(
        [
            jnp.concatenate([partner[0], partner[1]], axis=1),
            jnp.concatenate([partner[1], -partner[0]], axis=1),
        ],
        axis=0,
    )
    product = lax.dot_general(
        left_side, right_side, (((1,), (1,)), ((), ())), preferred_element_type=jnp.float32
    )
    real_part = product[:, :bands]
    imag_part = product[:, bands:]
    phases = jnp.arctan2(jnp.diagonal(imag_part), jnp.diagonal(real_part))
    coherence = jnp.sum(real_part * real_part + imag_part * imag_part) / bands
    return (phases, coherence)


def shards(coefficients, shift_blocks):
    planes = coefficients.shape[1]
    bands = coefficients.shape[4]
    width = coefficients.shape[5]
    own_planes = coefficients.reshape(2, planes, bands, width)
    shifts = shift_blocks * 128
    measure = jax.vmap(pair_measure, in_axes=(1, 1))
    next_first = passed_along(own_planes[:, 0], "kx", -1)
    x_wrap = lax.axis_index("kx") == lax.axis_size("kx") - 1
    next_first = jnp.where(x_wrap, jnp.roll(next_first, -shifts[0], axis=-1), next_first)
    x_partner = jnp.concatenate([own_planes[:, 1:], next_first[:, None]], axis=1)
    x_phases, x_coherence = measure(own_planes, x_partner)
    later = passed_along(own_planes, "ky", -1)
    y_wrap = lax.axis_index("ky") == lax.axis_size("ky") - 1
    y_partner = jnp.where(y_wrap, jnp.roll(later, -shifts[1], axis=-1), later)
    y_phases, y_coherence = measure(own_planes, y_partner)
    z_later = passed_along(own_planes, "kz", -1)
    z_wrap = lax.axis_index("kz") == lax.axis_size("kz") - 1
    z_partner = jnp.where(z_wrap, jnp.roll(z_later, -shifts[2], axis=-1), z_later)
    z_phases, z_coherence = measure(own_planes, z_partner)
    phases = jnp.stack([x_phases, y_phases, z_phases])
    coherence = jnp.stack([x_coherence, y_coherence, z_coherence]).reshape(3, planes, 1, 1)
    k_total = planes * lax.axis_size("kx") * lax.axis_size("ky") * lax.axis_size("kz")
    counts = jnp.array(
        [planes * lax.axis_size("kx"), lax.axis_size("ky"), lax.axis_size("kz")], jnp.float32
    )
    phase_sum = jnp.sum(phases, axis=1)
    totals, squares = lax.psum((phase_sum, jnp.sum(phases * phases, axis=1)), ("kx", "ky", "kz"))
    mean_phase = totals / k_total
    variance = squares / k_total - mean_phase * mean_phase
    centre = -counts[:, None] * mean_phase / (2.0 * jnp.pi)
    spread = (counts[:, None] / (2.0 * jnp.pi)) ** 2 * variance
    return (centre, spread, coherence)


def solution(mesh):
    in_specs = (P(None, "kx", "ky", "kz", None, None), P())
    out_specs = (P(), P(), P(None, "kx", "ky", "kz"))
    return jax.shard_map(shards, mesh=mesh, in_specs=in_specs, out_specs=out_specs, check_vma=False)
```

profile of v0, /device:TPU:0, one launch (start us, length us, event | category | flops | bytes accessed | tf_op | source)
XLA Modules:
  0.0 244.8 jit_solution(3515584299984125351)
XLA Ops:
  0.6 5.1 %collective-permute-start.2 = (bf16[2,1,512,2048]{3,2,0,1:T(8,128)(2,1)}, bf16[2,1,512,2048]{3,2,0,1:T(8,128)(2,1)}, u32[]{:S(2)}, u32[]{:S(2)}) collective-permute-start(bf16[2,1,512,2048]{3,2,0,1:T(8,128)(2,1)} %bitcast.83), channel_id=1, source_target_pairs={{0,3},{1,0},{2,1},{3,2},{4,7},{5,4},{6,5},{7,6},{8,11},{9,8},{10,9... | collective-permute-start | bytes 12582920 | tf_op jit(solution)/shard_map/ppermute | solution.py:10
  5.8 0.7 collective-permute-start.1
  6.4 1.5 collective-permute-start
  7.9 0.7 broadcast_multiply_fusion
  11.9 4.8 %slice_bitcast_fusion.5 = (bf16[1,512,2048]{2,1,0:T(8,128)(2,1)}, bf16[1,512,2048]{2,1,0:T(8,128)(2,1)}) fusion(bf16[2,1,1,1,512,2048]{5,4,3,2,1,0:T(8,128)(2,1)} %param.5), kind=kLoop, calls=%fused_computation.48 | loop fusion | bytes 8388608 | tf_op jit(solution)/shard_map/vmap()/squeeze;vmap()/transpose | solution.py:15
  16.6 79.3 %collective-permute-done.2 = bf16[2,1,512,2048]{3,2,0,1:T(8,128)(2,1)} collective-permute-done((bf16[2,1,512,2048]{3,2,0,1:T(8,128)(2,1)}, bf16[2,1,512,2048]{3,2,0,1:T(8,128)(2,1)}, u32[]{:S(2)}, u32[]{:S(2)}) %collective-permute-start.2) | collective-permute-done | bytes 4194336 | tf_op jit(solution)/shard_map/ppermute | solution.py:10
  95.9 6.5 %fusion.38 = bf16[2,1,512,2048]{3,2,1,0:T(8,128)(2,1)S(1)} fusion(bf16[2,1,512,2048]{3,2,0,1:T(8,128)(2,1)} %collective-permute-done.2, s32[]{:T(128)S(6)} %select_n.69, pred[]{:T(512)S(6)} %eq.15), kind=kLoop, calls=%fused_computation.77 | loop fusion | flops 10485760 | bytes 8388613 | tf_op jit(solution)/shard_map/jit(_where)/select_n | solution.py:51
  102.4 1.5 fusion.34
  103.8 1.6 slice_bitcast_fusion.1
  105.4 7.6 %fusion.37 = bf16[2,1,512,2048]{3,2,1,0:T(8,128)(2,1)S(1)} fusion(bf16[2,1,512,2048]{3,2,0,1:T(8,128)(2,1)} %collective-permute-done.1, s32[]{:T(128)S(6)} %select_n.67, pred[]{:T(512)S(6)} %eq.14), kind=kLoop, calls=%fused_computation.76 | loop fusion | flops 10485760 | bytes 8388613 | tf_op jit(solution)/shard_map/jit(_where)/select_n | solution.py:47
  113.0 1.5 fusion.33
  114.5 1.5 slice_bitcast_fusion.3
  116.0 6.5 %fusion.26 = bf16[2,512,2048]{2,1,0:T(8,128)(2,1)S(1)} fusion(bf16[2,512,2048]{2,1,0:T(8,128)(2,1)} %collective-permute-done, s32[]{:T(128)S(6)} %select_n.58, pred[]{:T(512)S(6)} %eq.13), kind=kLoop, calls=%fused_computation.41 | loop fusion | flops 10485760 | bytes 8388613 | tf_op jit(solution)/shard_map/jit(_where)/select_n | solution.py:42
  122.9 8.1 %fusion.29 = f32[1,512,1024]{2,1,0:T(8,128)} fusion(bf16[1,512,2048]{2,1,0:T(8,128)(2,1)S(1)} %get-tuple-element.7, bf16[1,512,2048]{2,1,0:T(8,128)(2,1)S(1)} %get-tuple-element.8, bf16[1,512,2048]{2,1,0:T(8,128)(2,1)S(1)} %get-tuple-element.6, bf16[1,512,2048]{2,1,0:T(8,128)(2,1)} %get-tuple-element.10, bf16[1,512,2048]{2,1,0:T(8,128)(2,1)} %get-tuple-element.9), kind=kOutput, calls=%fused_computation.51 | convolution fusion | flops 4336910336 | bytes 12582912 | tf_op jit(solution)/shard_map/vmap()/dot_general | solution.py:23
  131.0 2.5 %add_reduce_fusion.2 = (f32[]{:T(128)}, f32[512,512]{1,0:T(8,128)S(1)}, f32[512,512]{1,0:T(8,128)S(1)}) fusion(f32[1,512,1024]{2,1,0:T(8,128)} %fusion.29), kind=kLoop, calls=%fused_computation.54 | loop fusion | flops 1048575 | bytes 4194308 | tf_op jit(solution)/shard_map/vmap()/reduce_sum | solution.py:29
  133.5 4.5 %gather_fusion.1 = f32[512]{0:T(512)S(1)} fusion(f32[512,512]{1,0:T(8,128)S(1)} %get-tuple-element.12, s32[512]{0:T(512)S(1)} %bitcast.77), kind=kCustom, calls=%fused_computation.1 | custom fusion | bytes 8192 | tf_op jit(solution)/shard_map/vmap(jit(diagonal))/cond/branch_0_fun/gather | solution.py:28
  138.1 4.5 %gather_fusion = f32[512]{0:T(512)S(1)} fusion(f32[512,512]{1,0:T(8,128)S(1)} %get-tuple-element.13, s32[512]{0:T(512)S(1)} %bitcast.78), kind=kCustom, calls=%fused_computation | custom fusion | bytes 8192 | tf_op jit(solution)/shard_map/vmap(jit(diagonal))/cond/branch_0_fun/gather | solution.py:28
  142.6 6.5 %fusion.22 = bf16[2,1,512,2048]{3,2,0,1:T(8,128)(2,1)S(1)} fusion(bf16[2,1,512,2048]{3,2,0,1:T(8,128)(2,1)} %collective-permute-done.2, s32[]{:T(128)S(6)} %select_n.69, pred[]{:T(512)S(6)} %eq.15), kind=kLoop, calls=%fused_computation.37 | loop fusion | flops 10485760 | bytes 8388613 | tf_op jit(solution)/shard_map/jit(_where)/select_n | solution.py:51
  149.2 1.4 copy-done.2
  150.7 0.6 copy-done.3
  151.3 8.1 %fusion.27 = f32[1,512,1024]{2,1,0:T(8,128)} fusion(bf16[1,512,2048]{2,1,0:T(8,128)(2,1)S(1)} %copy-done.2, bf16[1,512,2048]{2,1,0:T(8,128)(2,1)S(1)} %slice_bitcast_fusion, bf16[1,512,2048]{2,1,0:T(8,128)(2,1)S(1)} %copy-done.3, bf16[1,512,2048]{2,1,0:T(8,128)(2,1)} %get-tuple-element.10, bf16[1,512,2048]{2,1,0:T(8,128)(2,1)} %get-tuple-element.9), kind=kOutput, calls=%fused_computation.49 | convolution fusion | flops 4336910336 | bytes 12582912 | tf_op jit(solution)/shard_map/vmap()/dot_general | solution.py:23
  159.4 2.5 %add_reduce_fusion = (f32[]{:T(128)}, f32[512,512]{1,0:T(8,128)S(1)}, f32[512,512]{1,0:T(8,128)S(1)}) fusion(f32[1,512,1024]{2,1,0:T(8,128)} %fusion.27), kind=kLoop, calls=%fused_computation.52 | loop fusion | flops 1048575 | bytes 4194308 | tf_op jit(solution)/shard_map/vmap()/reduce_sum | solution.py:29
  163.2 4.5 %gather_fusion.5 = f32[512]{0:T(512)S(1)} fusion(f32[512,512]{1,0:T(8,128)S(1)} %get-tuple-element.18, s32[512]{0:T(512)S(1)} %bitcast.79), kind=kCustom, calls=%fused_computation.5 | custom fusion | bytes 8192 | tf_op jit(solution)/shard_map/vmap(jit(diagonal))/cond/branch_0_fun/gather | solution.py:28
  167.7 4.5 %gather_fusion.4 = f32[512]{0:T(512)S(1)} fusion(f32[512,512]{1,0:T(8,128)S(1)} %get-tuple-element.19, s32[512]{0:T(512)S(1)} %bitcast.80), kind=kCustom, calls=%fused_computation.4 | custom fusion | bytes 8192 | tf_op jit(solution)/shard_map/vmap(jit(diagonal))/cond/branch_0_fun/gather | solution.py:28
  172.2 7.8 %fusion.24 = bf16[2,1,512,2048]{3,2,0,1:T(8,128)(2,1)S(1)} fusion(bf16[2,1,512,2048]{3,2,0,1:T(8,128)(2,1)} %collective-permute-done.1, s32[]{:T(128)S(6)} %select_n.67, pred[]{:T(512)S(6)} %eq.14), kind=kLoop, calls=%fused_computation.39 | loop fusion | flops 10485760 | bytes 8388613 | tf_op jit(solution)/shard_map/jit(_where)/select_n | solution.py:47
  180.2 1.4 copy-done
  182.3 8.1 %fusion.28 = f32[1,512,1024]{2,1,0:T(8,128)} fusion(bf16[1,512,2048]{2,1,0:T(8,128)(2,1)S(1)} %copy-done, bf16[1,512,2048]{2,1,0:T(8,128)(2,1)S(1)} %slice_bitcast_fusion.2, bf16[1,512,2048]{2,1,0:T(8,128)(2,1)S(1)} %copy-done.1, bf16[1,512,2048]{2,1,0:T(8,128)(2,1)} %get-tuple-element.10, bf16[1,512,2048]{2,1,0:T(8,128)(2,1)} %get-tuple-element.9), kind=kOutput, calls=%fused_computation.50 | convolution fusion | flops 4336910336 | bytes 12582912 | tf_op jit(solution)/shard_map/vmap()/dot_general | solution.py:23
  190.4 2.5 %add_reduce_fusion.1 = (f32[]{:T(128)}, f32[512,512]{1,0:T(8,128)S(1)}, f32[512,512]{1,0:T(8,128)S(1)}) fusion(f32[1,512,1024]{2,1,0:T(8,128)} %fusion.28), kind=kLoop, calls=%fused_computation.53 | loop fusion | flops 1048575 | bytes 4194308 | tf_op jit(solution)/shard_map/vmap()/reduce_sum | solution.py:29
  193.5 4.5 %gather_fusion.3 = f32[512]{0:T(512)S(1)} fusion(f32[512,512]{1,0:T(8,128)S(1)} %get-tuple-element.15, s32[512]{0:T(512)S(1)} %bitcast.81), kind=kCustom, calls=%fused_computation.3 | custom fusion | bytes 8192 | tf_op jit(solution)/shard_map/vmap(jit(diagonal))/cond/branch_0_fun/gather | solution.py:28
  198.1 4.5 %gather_fusion.2 = f32[512]{0:T(512)S(1)} fusion(f32[512,512]{1,0:T(8,128)S(1)} %get-tuple-element.16, s32[512]{0:T(512)S(1)} %bitcast.82), kind=kCustom, calls=%fused_computation.2 | custom fusion | bytes 8192 | tf_op jit(solution)/shard_map/vmap(jit(diagonal))/cond/branch_0_fun/gather | solution.py:28
  202.8 40.7 %all-reduce = (f32[3,512]{1,0:T(4,128)S(1)}, f32[3,512]{1,0:T(4,128)S(1)}) all-reduce(f32[3,512]{1,0:T(4,128)S(1)} %maximum_bitcast_fusion.16, f32[3,512]{1,0:T(4,128)S(1)} %maximum_multiply_fusion), channel_id=1, replica_groups=mesh['kx'=2,'ky'=4,'kz'=4] {'kx','ky','kz'}, use_global_device_ids=true, to_apply=%region_0.2 | all-reduce | flops 3072 | bytes 24576 | tf_op jit(solution)/shard_map/psum | solution.py:60
  244.1 0.7 subtract_multiply_fusion
  (22 shorter events, 2.6 us)
Async XLA Ops:
  0.6 95.3 %collective-permute-start.2 = (bf16[2,1,512,2048]{3,2,0,1:T(8,128)(2,1)}, bf16[2,1,512,2048]{3,2,0,1:T(8,128)(2,1)}, u32[]{:S(2)}, u32[]{:S(2)}) collective-permute-start(bf16[2,1,512,2048]{3,2,0,1:T(8,128)(2,1)} %bitcast.83), channel_id=1, source_target_pairs={{0,3},{1,0},{2,1},{3,2},{4,7},{5,4},{6,5},{7,6},{8,11},{9,8},{10,9... | collective-permute-start | bytes 12582920 | tf_op jit(solution)/shard_map/ppermute | solution.py:10
  5.8 99.7 %collective-permute-start.1 = (bf16[2,1,512,2048]{3,2,0,1:T(8,128)(2,1)}, bf16[2,1,512,2048]{3,2,0,1:T(8,128)(2,1)}, u32[]{:S(2)}, u32[]{:S(2)}) collective-permute-start(bf16[2,1,512,2048]{3,2,0,1:T(8,128)(2,1)} %bitcast.84), channel_id=1, source_target_pairs={{0,12},{4,0},{8,4},{12,8},{1,13},{5,1},{9,5},{13,9},{2,14},{6,2},{... | collective-permute-start | bytes 12582920 | tf_op jit(solution)/shard_map/ppermute | solution.py:10
  6.4 109.6 %collective-permute-start = (bf16[2,512,2048]{2,1,0:T(8,128)(2,1)}, bf16[2,512,2048]{2,1,0:T(8,128)(2,1)}, u32[]{:S(2)}, u32[]{:S(2)}) collective-permute-start(bf16[2,512,2048]{2,1,0:T(8,128)(2,1)} %bitcast.85), channel_id=1, source_target_pairs={{0,16},{16,0},{1,17},{17,1},{2,18},{18,2},{3,19},{19,3},{4,20},{20... | collective-permute-start | bytes 12582920 | tf_op jit(solution)/shard_map/ppermute | solution.py:10
  149.1 1.6 copy-start.2
  149.1 2.2 copy-start.3
  180.0 1.6 copy-start
  180.0 2.2 copy-start.1
  190.4 53.7 %copy-start.4 = (f32[3]{0:T(128)S(1)}, f32[3]{0:T(128)}, u32[]{:S(2)}) copy-start(f32[3]{0:T(128)} %constant.98) | copy-start | bytes 40
  190.4 53.7 %copy-start.5 = (f32[3]{0:T(128)S(1)}, f32[3]{0:T(128)}, u32[]{:S(2)}) copy-start(f32[3]{0:T(128)} %constant.95) | copy-start | bytes 40
where the time goes:
time: 245 us
  waiting for transfers between devices  79.3 us (32%)
  other arithmetic  47.5 us (19%)
  blocking collectives  40.7 us (17%)
  local copies, waits for them, and re-layouts  40.1 us (16%)
  matrix products  24.3 us (10%)
  starting transfers between devices  7.3 us (3%)
  between operations  5.43 us (2%)
    ppermute x3, waiting for transfers between devices, passed_along(): return lax.ppermute(value, axis, pairs)  79.3 us
    psum x1, blocking collectives, shards(): lax.psum((phase_sum, jnp.sum(phases * phases, axis=1)), ('kx', 'ky', 'kz'))  40.7 us
    gather x6, local copies, waits for them, and re-layouts, pair_measure(): phases = jnp.arctan2(jnp.diagonal(imag_part), jnp.diagonal(real_part))  27.1 us
    dot_general x3, matrix products, pair_measure(): lax.dot_general(left_side, right_side, (((1,), (1,)), ((), ())), preferre...  24.3 us
    select_n x2, other arithmetic, shards(): y_partner = jnp.where(y_wrap, jnp.roll(later, -shifts[1], axis=-1), later)  15.3 us
    select_n x2, other arithmetic, shards(): jnp.where(z_wrap, jnp.roll(z_later, -shifts[2], axis=-1), z_later)  12.9 us
    reduce_sum x3, other arithmetic, pair_measure(): coherence = jnp.sum(real_part * real_part + imag_part * imag_part) / bands  7.5 us
    ppermute x3, starting transfers between devices, passed_along(): return lax.ppermute(value, axis, pairs)  7.3 us
  transfers between devices with their start and end apart: 3, of which 1 were waited for; matrix products, arithmetic and copies ran while one was open for 11% of the time, Pallas kernels for 0%

commit v1 on v0

--- a/solution.py
+++ b/solution.py
@@ -57,7 +57,9 @@
         [planes * lax.axis_size("kx"), lax.axis_size("ky"), lax.axis_size("kz")], jnp.float32
     )
     phase_sum = jnp.sum(phases, axis=1)
-    totals, squares = lax.psum((phase_sum, jnp.sum(phases * phases, axis=1)), ("kx", "ky", "kz"))
+    totals, squares = lax.psum(
+        lax.psum((phase_sum, jnp.sum(phases * phases, axis=1)), ("ky", "kz")), "kx"
+    )
     mean_phase = totals / k_total
     variance = squares / k_total - mean_phase * mean_phase
     centre = -counts[:, None] * mean_phase / (2.0 * jnp.pi)

time: 245 us -> 274 us (1.12)
  blocking collectives: 40.7 us -> 69.8 us
    psum x1 -> x2, blocking collectives: 40.7 us -> 69.8 us  [the longest x1 61.7 us: shards(): lax.psum((phase_sum, jnp.sum(phases * phases, axis=1)), ('ky', 'kz'))]
  transfers between devices with their start and end apart: 3 -> 3, of which waited for: 1 -> 1; matrix products, arithmetic and copies ran while one was open for 11% -> 10% of each run, Pallas kernels for 0% -> 0%
where the time goes in v1:
time: 274 us
  waiting for transfers between devices  79.3 us (29%)
  blocking collectives  69.8 us (25%)
  other arithmetic  47.4 us (17%)
  local copies, waits for them, and re-layouts  40.1 us (15%)
  matrix products  24.3 us (9%)
  starting transfers between devices  7.3 us (3%)
  between operations  5.43 us (2%)
    ppermute x3, waiting for transfers between devices, passed_along(): return lax.ppermute(value, axis, pairs)  79.3 us
    psum x1, blocking collectives, shards(): lax.psum((phase_sum, jnp.sum(phases * phases, axis=1)), ('ky', 'kz'))  61.7 us
    gather x6, local copies, waits for them, and re-layouts, pair_measure(): phases = jnp.arctan2(jnp.diagonal(imag_part), jnp.diagonal(real_part))  27.1 us
    dot_general x3, matrix products, pair_measure(): lax.dot_general(left_side, right_side, (((1,), (1,)), ((), ())), preferre...  24.3 us
    select_n x2, other arithmetic, shards(): y_partner = jnp.where(y_wrap, jnp.roll(later, -shifts[1], axis=-1), later)  15.2 us
    select_n x2, other arithmetic, shards(): jnp.where(z_wrap, jnp.roll(z_later, -shifts[2], axis=-1), z_later)  12.9 us
    psum x1, blocking collectives, shards(): lax.psum(lax.psum((phase_sum, jnp.sum(phases * phases, axis=1)), ('ky', '...  8.08 us
    reduce_sum x3, other arithmetic, pair_measure(): coherence = jnp.sum(real_part * real_part + imag_part * imag_part) / bands  7.5 us
  transfers between devices with their start and end apart: 3, of which 1 were waited for; matrix products, arithmetic and copies ran while one was open for 10% of the time, Pallas kernels for 0%

profile of v1, /device:TPU:0, one launch (start us, length us, event | category | flops | bytes accessed | tf_op | source)
XLA Modules:
  0.0 273.6 jit_solution(15502830539365730436)
XLA Ops:
  0.6 5.1 %collective-permute-start.2 = (bf16[2,1,512,2048]{3,2,0,1:T(8,128)(2,1)}, bf16[2,1,512,2048]{3,2,0,1:T(8,128)(2,1)}, u32[]{:S(2)}, u32[]{:S(2)}) collective-permute-start(bf16[2,1,512,2048]{3,2,0,1:T(8,128)(2,1)} %bitcast.83), channel_id=1, source_target_pairs={{0,3},{1,0},{2,1},{3,2},{4,7},{5,4},{6,5},{7,6},{8,11},{9,8},{10,9... | collective-permute-start | bytes 12582920 | tf_op jit(solution)/shard_map/ppermute | solution.py:10
  5.8 0.7 collective-permute-start.1
  6.4 1.5 collective-permute-start
  7.9 0.7 broadcast_multiply_fusion
  11.9 4.7 %slice_bitcast_fusion.5 = (bf16[1,512,2048]{2,1,0:T(8,128)(2,1)}, bf16[1,512,2048]{2,1,0:T(8,128)(2,1)}) fusion(bf16[2,1,1,1,512,2048]{5,4,3,2,1,0:T(8,128)(2,1)} %param.5), kind=kLoop, calls=%fused_computation.48 | loop fusion | bytes 8388608 | tf_op jit(solution)/shard_map/vmap()/squeeze;vmap()/transpose | solution.py:15
  16.6 79.3 %collective-permute-done.2 = bf16[2,1,512,2048]{3,2,0,1:T(8,128)(2,1)} collective-permute-done((bf16[2,1,512,2048]{3,2,0,1:T(8,128)(2,1)}, bf16[2,1,512,2048]{3,2,0,1:T(8,128)(2,1)}, u32[]{:S(2)}, u32[]{:S(2)}) %collective-permute-start.2) | collective-permute-done | bytes 4194336 | tf_op jit(solution)/shard_map/ppermute | solution.py:10
  95.9 6.5 %fusion.38 = bf16[2,1,512,2048]{3,2,1,0:T(8,128)(2,1)S(1)} fusion(bf16[2,1,512,2048]{3,2,0,1:T(8,128)(2,1)} %collective-permute-done.2, s32[]{:T(128)S(6)} %select_n.69, pred[]{:T(512)S(6)} %eq.15), kind=kLoop, calls=%fused_computation.77 | loop fusion | flops 10485760 | bytes 8388613 | tf_op jit(solution)/shard_map/jit(_where)/select_n | solution.py:51
  102.4 1.4 fusion.34
  103.8 1.6 slice_bitcast_fusion.1
  105.4 7.5 %fusion.37 = bf16[2,1,512,2048]{3,2,1,0:T(8,128)(2,1)S(1)} fusion(bf16[2,1,512,2048]{3,2,0,1:T(8,128)(2,1)} %collective-permute-done.1, s32[]{:T(128)S(6)} %select_n.67, pred[]{:T(512)S(6)} %eq.14), kind=kLoop, calls=%fused_computation.76 | loop fusion | flops 10485760 | bytes 8388613 | tf_op jit(solution)/shard_map/jit(_where)/select_n | solution.py:47
  112.9 1.5 fusion.33
  114.4 1.6 slice_bitcast_fusion.3
  115.9 6.5 %fusion.26 = bf16[2,512,2048]{2,1,0:T(8,128)(2,1)S(1)} fusion(bf16[2,512,2048]{2,1,0:T(8,128)(2,1)} %collective-permute-done, s32[]{:T(128)S(6)} %select_n.58, pred[]{:T(512)S(6)} %eq.13), kind=kLoop, calls=%fused_computation.41 | loop fusion | flops 10485760 | bytes 8388613 | tf_op jit(solution)/shard_map/jit(_where)/select_n | solution.py:42
  122.8 8.1 %fusion.29 = f32[1,512,1024]{2,1,0:T(8,128)} fusion(bf16[1,512,2048]{2,1,0:T(8,128)(2,1)S(1)} %get-tuple-element.9, bf16[1,512,2048]{2,1,0:T(8,128)(2,1)S(1)} %get-tuple-element.10, bf16[1,512,2048]{2,1,0:T(8,128)(2,1)S(1)} %get-tuple-element.8, bf16[1,512,2048]{2,1,0:T(8,128)(2,1)} %get-tuple-element.12, bf16[1,512,2048]{2,1,0:T(8,128)(2,1)} %get-tuple-element.11), kind=kOutput, calls=%fused_computation.51 | convolution fusion | flops 4336910336 | bytes 12582912 | tf_op jit(solution)/shard_map/vmap()/dot_general | solution.py:23
  130.9 2.5 add_reduce_fusion.2
  133.4 4.5 %gather_fusion.1 = f32[512]{0:T(512)S(1)} fusion(f32[512,512]{1,0:T(8,128)S(1)} %get-tuple-element.14, s32[512]{0:T(512)S(1)} %bitcast.77), kind=kCustom, calls=%fused_computation.1 | custom fusion | bytes 8192 | tf_op jit(solution)/shard_map/vmap(jit(diagonal))/cond/branch_0_fun/gather | solution.py:28
  138.0 4.5 %gather_fusion = f32[512]{0:T(512)S(1)} fusion(f32[512,512]{1,0:T(8,128)S(1)} %get-tuple-element.15, s32[512]{0:T(512)S(1)} %bitcast.78), kind=kCustom, calls=%fused_computation | custom fusion | bytes 8192 | tf_op jit(solution)/shard_map/vmap(jit(diagonal))/cond/branch_0_fun/gather | solution.py:28
  142.5 6.5 %fusion.22 = bf16[2,1,512,2048]{3,2,0,1:T(8,128)(2,1)S(1)} fusion(bf16[2,1,512,2048]{3,2,0,1:T(8,128)(2,1)} %collective-permute-done.2, s32[]{:T(128)S(6)} %select_n.69, pred[]{:T(512)S(6)} %eq.15), kind=kLoop, calls=%fused_computation.37 | loop fusion | flops 10485760 | bytes 8388613 | tf_op jit(solution)/shard_map/jit(_where)/select_n | solution.py:51
  149.1 1.4 copy-done.2
  151.2 8.1 %fusion.27 = f32[1,512,1024]{2,1,0:T(8,128)} fusion(bf16[1,512,2048]{2,1,0:T(8,128)(2,1)S(1)} %copy-done.2, bf16[1,512,2048]{2,1,0:T(8,128)(2,1)S(1)} %slice_bitcast_fusion, bf16[1,512,2048]{2,1,0:T(8,128)(2,1)S(1)} %copy-done.3, bf16[1,512,2048]{2,1,0:T(8,128)(2,1)} %get-tuple-element.12, bf16[1,512,2048]{2,1,0:T(8,128)(2,1)} %get-tuple-element.11), kind=kOutput, calls=%fused_computation.49 | convolution fusion | flops 4336910336 | bytes 12582912 | tf_op jit(solution)/shard_map/vmap()/dot_general | solution.py:23
  159.3 2.5 add_reduce_fusion
  163.1 4.5 %gather_fusion.5 = f32[512]{0:T(512)S(1)} fusion(f32[512,512]{1,0:T(8,128)S(1)} %get-tuple-element.20, s32[512]{0:T(512)S(1)} %bitcast.79), kind=kCustom, calls=%fused_computation.5 | custom fusion | bytes 8192 | tf_op jit(solution)/shard_map/vmap(jit(diagonal))/cond/branch_0_fun/gather | solution.py:28
  167.6 4.5 %gather_fusion.4 = f32[512]{0:T(512)S(1)} fusion(f32[512,512]{1,0:T(8,128)S(1)} %get-tuple-element.21, s32[512]{0:T(512)S(1)} %bitcast.80), kind=kCustom, calls=%fused_computation.4 | custom fusion | bytes 8192 | tf_op jit(solution)/shard_map/vmap(jit(diagonal))/cond/branch_0_fun/gather | solution.py:28
  172.1 7.7 %fusion.24 = bf16[2,1,512,2048]{3,2,0,1:T(8,128)(2,1)S(1)} fusion(bf16[2,1,512,2048]{3,2,0,1:T(8,128)(2,1)} %collective-permute-done.1, s32[]{:T(128)S(6)} %select_n.67, pred[]{:T(512)S(6)} %eq.14), kind=kLoop, calls=%fused_computation.39 | loop fusion | flops 10485760 | bytes 8388613 | tf_op jit(solution)/shard_map/jit(_where)/select_n | solution.py:47
  180.0 1.4 copy-done
  182.1 8.1 %fusion.28 = f32[1,512,1024]{2,1,0:T(8,128)} fusion(bf16[1,512,2048]{2,1,0:T(8,128)(2,1)S(1)} %copy-done, bf16[1,512,2048]{2,1,0:T(8,128)(2,1)S(1)} %slice_bitcast_fusion.2, bf16[1,512,2048]{2,1,0:T(8,128)(2,1)S(1)} %copy-done.1, bf16[1,512,2048]{2,1,0:T(8,128)(2,1)} %get-tuple-element.12, bf16[1,512,2048]{2,1,0:T(8,128)(2,1)} %get-tuple-element.11), kind=kOutput, calls=%fused_computation.50 | convolution fusion | flops 4336910336 | bytes 12582912 | tf_op jit(solution)/shard_map/vmap()/dot_general | solution.py:23
  190.2 2.5 add_reduce_fusion.1
  193.3 4.5 %gather_fusion.3 = f32[512]{0:T(512)S(1)} fusion(f32[512,512]{1,0:T(8,128)S(1)} %get-tuple-element.17, s32[512]{0:T(512)S(1)} %bitcast.81), kind=kCustom, calls=%fused_computation.3 | custom fusion | bytes 8192 | tf_op jit(solution)/shard_map/vmap(jit(diagonal))/cond/branch_0_fun/gather | solution.py:28
  197.9 4.5 %gather_fusion.2 = f32[512]{0:T(512)S(1)} fusion(f32[512,512]{1,0:T(8,128)S(1)} %get-tuple-element.18, s32[512]{0:T(512)S(1)} %bitcast.82), kind=kCustom, calls=%fused_computation.2 | custom fusion | bytes 8192 | tf_op jit(solution)/shard_map/vmap(jit(diagonal))/cond/branch_0_fun/gather | solution.py:28
  202.6 61.7 %all-reduce = (f32[3,512]{1,0:T(4,128)S(1)}, f32[3,512]{1,0:T(4,128)S(1)}) all-reduce(f32[3,512]{1,0:T(4,128)S(1)} %maximum_bitcast_fusion.16, f32[3,512]{1,0:T(4,128)S(1)} %maximum_multiply_fusion), channel_id=1, replica_groups=mesh['kx'=2,'ky'=4,'kz'=4] {'ky','kz'}, use_global_device_ids=true, to_apply=%region_0.2 | all-reduce | flops 3072 | bytes 24576 | tf_op jit(solution)/shard_map/psum | solution.py:61
  264.3 8.1 %all-reduce.1 = (f32[3,512]{1,0:T(4,128)S(1)}, f32[3,512]{1,0:T(4,128)S(1)}) all-reduce(f32[3,512]{1,0:T(4,128)S(1)} %get-tuple-element.4, f32[3,512]{1,0:T(4,128)S(1)} %get-tuple-element.5), channel_id=1, replica_groups=mesh['kx'=2,'ky'=4,'kz'=4] {'kx'}, use_global_device_ids=true, to_apply=%region_1.3 | all-reduce | flops 3072 | bytes 24576 | tf_op jit(solution)/shard_map/psum | solution.py:60
  272.9 0.7 subtract_multiply_fusion
  (23 shorter events, 3.3 us)
Async XLA Ops:
  0.6 95.3 %collective-permute-start.2 = (bf16[2,1,512,2048]{3,2,0,1:T(8,128)(2,1)}, bf16[2,1,512,2048]{3,2,0,1:T(8,128)(2,1)}, u32[]{:S(2)}, u32[]{:S(2)}) collective-permute-start(bf16[2,1,512,2048]{3,2,0,1:T(8,128)(2,1)} %bitcast.83), channel_id=1, source_target_pairs={{0,3},{1,0},{2,1},{3,2},{4,7},{5,4},{6,5},{7,6},{8,11},{9,8},{10,9... | collective-permute-start | bytes 12582920 | tf_op jit(solution)/shard_map/ppermute | solution.py:10
  5.8 99.7 %collective-permute-start.1 = (bf16[2,1,512,2048]{3,2,0,1:T(8,128)(2,1)}, bf16[2,1,512,2048]{3,2,0,1:T(8,128)(2,1)}, u32[]{:S(2)}, u32[]{:S(2)}) collective-permute-start(bf16[2,1,512,2048]{3,2,0,1:T(8,128)(2,1)} %bitcast.84), channel_id=1, source_target_pairs={{0,12},{4,0},{8,4},{12,8},{1,13},{5,1},{9,5},{13,9},{2,14},{6,2},{... | collective-permute-start | bytes 12582920 | tf_op jit(solution)/shard_map/ppermute | solution.py:10
  6.4 109.5 %collective-permute-start = (bf16[2,512,2048]{2,1,0:T(8,128)(2,1)}, bf16[2,512,2048]{2,1,0:T(8,128)(2,1)}, u32[]{:S(2)}, u32[]{:S(2)}) collective-permute-start(bf16[2,512,2048]{2,1,0:T(8,128)(2,1)} %bitcast.85), channel_id=1, source_target_pairs={{0,16},{16,0},{1,17},{17,1},{2,18},{18,2},{3,19},{19,3},{4,20},{20... | collective-permute-start | bytes 12582920 | tf_op jit(solution)/shard_map/ppermute | solution.py:10
  149.0 1.6 copy-start.2
  149.0 2.2 copy-start.3
  179.9 1.6 copy-start
  179.9 2.2 copy-start.1
  190.2 82.8 %copy-start.4 = (f32[3]{0:T(128)S(1)}, f32[3]{0:T(128)}, u32[]{:S(2)}) copy-start(f32[3]{0:T(128)} %constant.98) | copy-start | bytes 40
  190.2 82.8 %copy-start.5 = (f32[3]{0:T(128)S(1)}, f32[3]{0:T(128)}, u32[]{:S(2)}) copy-start(f32[3]{0:T(128)} %constant.95) | copy-start | bytes 40
